TPU v7x, 32 devices: a whole 2x2x4 slice. The times are simulated.
32 devices in a mesh: dp: 8 (over z, y), head: 4 (over x, core).
Axes of the slice: x: 2, y: 2, z: 4, core: 2. Of those that a mesh axis runs over, the one named last changes fastest.
Arguments:
- tokens: bfloat16 [8, 6312, 768], P('dp', 'head'), may hold values from -6 to 6
- frames: int32 [8], P('dp'), may hold values from 4 to 16
- text_mask: int32 [8, 40], P('dp'), may hold values 0 or 1
- latents: bfloat16 [8, 128, 768], P('dp'), may hold values from -6 to 6
- cross_q: bfloat16 [768, 768], P('head'), may hold values from -0.21875 to 0.21875
- cross_kv: bfloat16 [2, 768, 768], P(None, 'head'), may hold values from -0.21875 to 0.21875
- cross_out: bfloat16 [768, 768], P('head'), may hold values from -3.5 to 3.5
- cross_up: bfloat16 [768, 3072], P(None, 'head'), may hold values from -0.21875 to 0.21875
- cross_down: bfloat16 [3072, 768], P('head'), may hold values from -0.109375 to 0.109375
- self_qkv: bfloat16 [3, 768, 768], P(None, 'head'), may hold values from -0.21875 to 0.21875
- self_out: bfloat16 [768, 768], P('head'), may hold values from -0.875 to 0.875
- self_up: bfloat16 [768, 3072], P(None, 'head'), may hold values from -0.21875 to 0.21875
- self_down: bfloat16 [3072, 768], P('head'), may hold values from -0.109375 to 0.109375
- head_bias: float32 [2, 2, 768], P(None, None, 'head'), may hold values from -1.8 to 1.8
- up_bias: float32 [2, 3072], P(None, 'head'), may hold values from -1.8 to 1.8
- out_bias: float32 [2, 2, 768], replicated, may hold values from -1.8 to 1.8
- norm_gain: float32 [5, 768], replicated, may hold values from 0.5 to 1.5
- norm_bias: float32 [5, 768], replicated, may hold values from -1.8 to 1.8
- latents_cot: float32 [8, 128, 768], P('dp'), may hold values from -6 to 6
Outputs:
- latents_out: float32 [8, 128, 768], P('dp')
- grad_tokens: bfloat16 [8, 6312, 768], P('dp', 'head')
- grad_latents: float32 [8, 128, 768], P('dp')
- grad_cross_q: float32 [768, 768], P('head', 'dp')
- grad_cross_kv: float32 [2, 768, 768], P(None, 'head', 'dp')
- grad_cross_out: float32 [768, 768], P('head', 'dp')
- grad_cross_up: float32 [768, 3072], P('dp', 'head')
- grad_cross_down: float32 [3072, 768], P('head', 'dp')
- grad_self_qkv: float32 [3, 768, 768], P(None, 'head', 'dp')
- grad_self_out: float32 [768, 768], P('head', 'dp')
- grad_self_up: float32 [768, 3072], P('dp', 'head')
- grad_self_down: float32 [3072, 768], P('head', 'dp')
- grad_head_bias: float32 [2, 2, 768], P(None, None, 'head')
- grad_up_bias: float32 [2, 3072], P(None, 'head')
- grad_out_bias: float32 [2, 2, 768], P(None, None, 'head')
- grad_norm_gain: float32 [5, 768], P(None, 'head')
- grad_norm_bias: float32 [5, 768], P(None, 'head')
Inputs may be any that keep to these rules, and one draw needn't show every extreme that they name: The patches of frames at or after frames[c] are padding.
All inputs are finite; a program needn't handle non-finite values. No bound on the sum of `text_mask` on one device may be relied on, other than what follows from the above.
Results may differ from a plain program's by a relative error of at most 0.018.
Values may be sent and summed in bfloat16 or wider, within the bound.
A program may use at most 128 MiB of HBM per device.

v0:
```python
from functools import partial
import jax
import jax.numpy as jnp
from jax import lax
from jax.sharding import PartitionSpec as P

HD = 64
P_SIZE = 392
F_MAX = 16
EPSILON = 1e-05
NEGATIVE = -1e30


def normed(tensor, gain_row, shift_row):
    row_mean = jnp.mean(tensor, axis=-1, keepdims=True)
    centered = tensor - row_mean
    spread = jnp.mean(centered * centered, axis=-1, keepdims=True)
    return centered * lax.rsqrt(spread + EPSILON) * gain_row + shift_row


def share_of(tensor, head_index, head_width):
    return lax.dynamic_slice_in_dim(tensor, head_index * head_width, head_width, tensor.ndim - 1)


def split_heads(tensor, heads_here):
    return tensor.reshape(
        tensor.shape[0], tensor.shape[1], heads_here, tensor.shape[2] // heads_here
    )


def merge_heads(tensor):
    return tensor.reshape(tensor.shape[0], tensor.shape[1], tensor.shape[2] * tensor.shape[3])


def join_heads(partial_sum):
    return lax.psum(partial_sum.astype(jnp.bfloat16), "head").astype(jnp.float32)


def join_back(partial_sum):
    return lax.psum(partial_sum.astype(jnp.bfloat16), "head").astype(jnp.float32)


def scores_of(queries, key_rows, usable):
    scores = jnp.einsum("qhe,khe->hqk", queries, key_rows, preferred_element_type=jnp.float32)
    return jnp.where(usable[None, None, :], scores, NEGATIVE)


def attend_parts(parts):
    queries, key_rows, values, usable = parts
    scores = scores_of(queries, key_rows, usable)
    row_max = jnp.max(scores, axis=-1, keepdims=True)
    powers = jnp.exp(scores - row_max)
    totals = jnp.sum(powers, axis=-1, keepdims=True)
    chances = (powers / totals).astype(jnp.bfloat16)
    mixture = jnp.einsum("hqk,khe->qhe", chances, values, preferred_element_type=jnp.float32)
    return (mixture.astype(jnp.bfloat16), row_max, totals)


def back_parts(parts):
    queries, key_rows, values, usable, row_max, totals, grad_mix = parts
    scores = scores_of(queries, key_rows, usable)
    chances = jnp.exp(scores - row_max) / totals
    rounded = chances.astype(jnp.bfloat16)
    grad_values = jnp.einsum(
        "hqk,qhe->khe", rounded, grad_mix, preferred_element_type=jnp.float32
    ).astype(jnp.bfloat16)
    grad_chances = jnp.einsum("qhe,khe->hqk", grad_mix, values, preferred_element_type=jnp.float32)
    inner_sum = jnp.sum(chances * grad_chances, axis=-1, keepdims=True)
    grad_scores = (chances * (grad_chances - inner_sum)).astype(jnp.bfloat16)
    grad_queries = jnp.einsum(
        "hqk,khe->qhe", grad_scores, key_rows, preferred_element_type=jnp.float32
    ).astype(jnp.bfloat16)
    grad_keys = jnp.einsum(
        "hqk,qhe->khe", grad_scores, queries, preferred_element_type=jnp.float32
    ).astype(jnp.bfloat16)
    return (grad_queries, grad_keys, grad_values)


def feed_forward(tensor, gain_row, shift_row, weight_up, bias_up, weight_down):
    hidden = normed(tensor, gain_row, shift_row).astype(jnp.bfloat16)
    pre_act = (
        jnp.einsum("cnd,df->cnf", hidden, weight_up, preferred_element_type=jnp.float32) + bias_up
    )
    activation = jax.nn.gelu(pre_act, approximate=True).astype(jnp.bfloat16)
    partial_sum = jnp.einsum(
        "cnf,fd->cnd", activation, weight_down, preferred_element_type=jnp.float32
    )
    return (join_heads(partial_sum), (hidden, pre_act, activation))


def feed_back(tensor, gain_row, shift_row, weight_up, weight_down, saved_acts, grad_out):
    hidden, pre_act, activation = saved_acts
    grad_branch = grad_out.astype(jnp.bfloat16)
    grad_weight_down = jnp.einsum(
        "cnf,cnd->fd", activation, grad_branch, preferred_element_type=jnp.float32
    )
    grad_act = jnp.einsum(
        "cnd,fd->cnf", grad_branch, weight_down, preferred_element_type=jnp.float32
    )
    unused, gelu_pull = jax.vjp(partial(jax.nn.gelu, approximate=True), pre_act)
    grad_pre = gelu_pull(grad_act)[0].astype(jnp.bfloat16)
    grad_weight_up = jnp.einsum("cnd,cnf->df", hidden, grad_pre, preferred_element_type=jnp.float32)
    grad_bias_up = jnp.sum(grad_pre.astype(jnp.float32), axis=(0, 1))
    grad_hidden = join_back(
        jnp.einsum("cnf,df->cnd", grad_pre, weight_up, preferred_element_type=jnp.float32)
    )
    unused_too, norm_pull = jax.vjp(normed, tensor, gain_row, shift_row)
    grad_tensor, grad_gain, grad_shift = norm_pull(grad_hidden)
    return (grad_tensor, grad_weight_up, grad_bias_up, grad_weight_down, grad_gain, grad_shift)


def local(
    tokens,
    frames,
    text_mask,
    latents,
    cross_q,
    cross_kv,
    cross_out,
    cross_up,
    cross_down,
    self_qkv,
    self_out,
    self_up,
    self_down,
    head_bias,
    up_bias,
    out_bias,
    norm_gain,
    norm_bias,
    latents_cot,
):
    head_index = lax.axis_index("head")
    head_width = cross_q.shape[0]
    heads_here = head_width // HD
    scaling = HD ** (-0.5)
    clips_here = tokens.shape[0]
    rows_here = tokens.shape[1]
    length = rows_here * lax.axis_size("head")
    position = jnp.arange(length, dtype=jnp.int32)
    text_full = jnp.concatenate(
        [jnp.zeros((clips_here, F_MAX * P_SIZE), jnp.int32), text_mask], axis=1
    )
    usable = (position[None, :] < frames[:, None] * P_SIZE) | (text_full == 1)
    gathered, weights_whole = (
        lax.all_gather(tokens, "head", axis=1, tiled=True),
        lax.all_gather(cross_kv, "head", axis=1, tiled=True),
    )
    full_rows = gathered.astype(jnp.float32)
    row_mean = jnp.mean(full_rows, axis=-1, keepdims=True)
    centered = full_rows - row_mean
    inverse = lax.rsqrt(jnp.mean(centered * centered, axis=-1, keepdims=True) + EPSILON)
    inputs = (centered * inverse * norm_gain[0] + norm_bias[0]).astype(jnp.bfloat16)
    key_value = jnp.einsum("cld,kwd->clkw", inputs, cross_kv, preferred_element_type=jnp.float32)
    key_rows = key_value[:, :, 0].astype(jnp.bfloat16)
    cross_values = (key_value[:, :, 1] + head_bias[0, 1]).astype(jnp.bfloat16)
    start_state = latents.astype(jnp.float32)
    latent_norm = normed(start_state, norm_gain[1], norm_bias[1]).astype(jnp.bfloat16)
    cross_queries = (
        (
            jnp.einsum("cnd,wd->cnw", latent_norm, cross_q, preferred_element_type=jnp.float32)
            + head_bias[0, 0]
        )
        * scaling
    ).astype(jnp.bfloat16)
    cross_parts = (
        split_heads(cross_queries, heads_here),
        split_heads(key_rows, heads_here),
        split_heads(cross_values, heads_here),
        usable,
    )
    cross_mix, cross_max, cross_totals = lax.map(attend_parts, cross_parts)
    cross_flat = merge_heads(cross_mix)
    after_cross = (
        start_state
        + join_heads(
            jnp.einsum("cnw,wd->cnd", cross_flat, cross_out, preferred_element_type=jnp.float32)
        )
        + out_bias[0, 0]
    )
    cross_branch, cross_saved = feed_forward(
        after_cross, norm_gain[2], norm_bias[2], cross_up, up_bias[0], cross_down
    )
    after_mlp = after_cross + cross_branch + out_bias[0, 1]
    self_norm = normed(after_mlp, norm_gain[3], norm_bias[3]).astype(jnp.bfloat16)
    triple = jnp.einsum("cnd,kwd->cnkw", self_norm, self_qkv, preferred_element_type=jnp.float32)
    self_queries = ((triple[:, :, 0] + head_bias[1, 0]) * scaling).astype(jnp.bfloat16)
    self_keys = triple[:, :, 1].astype(jnp.bfloat16)
    self_values = (triple[:, :, 2] + head_bias[1, 1]).astype(jnp.bfloat16)
    everyone = jnp.ones((clips_here, self_keys.shape[1]), dtype=bool)
    self_parts = (
        split_heads(self_queries, heads_here),
        split_heads(self_keys, heads_here),
        split_heads(self_values, heads_here),
        everyone,
    )
    self_mix, self_max, self_totals = lax.map(attend_parts, self_parts)
    self_flat = merge_heads(self_mix)
    after_self = (
        after_mlp
        + join_heads(
            jnp.einsum("cnw,wd->cnd", self_flat, self_out, preferred_element_type=jnp.float32)
        )
        + out_bias[1, 0]
    )
    self_branch, self_saved = feed_forward(
        after_self, norm_gain[4], norm_bias[4], self_up, up_bias[1], self_down
    )
    latents_out = after_self + self_branch + out_bias[1, 1]
    bias_self_mlp = jnp.sum(latents_cot, axis=(0, 1))
    grad_ln_four, grad_self_up, upbias_self, grad_self_down, gain_four, shift_four = feed_back(
        after_self, norm_gain[4], norm_bias[4], self_up, self_down, self_saved, latents_cot
    )
    grad_state = latents_cot + grad_ln_four
    bias_self_attn = jnp.sum(grad_state, axis=(0, 1))
    grad_attn_in = grad_state.astype(jnp.bfloat16)
    grad_self_out = jnp.einsum(
        "cnw,cnd->wd", self_flat, grad_attn_in, preferred_element_type=jnp.float32
    )
    grad_mix = jnp.einsum(
        "cnd,wd->cnw", grad_attn_in, self_out, preferred_element_type=jnp.float32
    ).astype(jnp.bfloat16)
    self_grads = lax.map(
        back_parts, self_parts + (self_max, self_totals, split_heads(grad_mix, heads_here))
    )
    grad_query_scaled = (merge_heads(self_grads[0]).astype(jnp.float32) * scaling).astype(
        jnp.bfloat16
    )
    grad_triple = jnp.stack(
        [grad_query_scaled, merge_heads(self_grads[1]), merge_heads(self_grads[2])], axis=2
    )
    grad_self_qkv = jnp.einsum(
        "cnd,cnkw->kwd", self_norm, grad_triple, preferred_element_type=jnp.float32
    )
    bias_self_q = jnp.sum(grad_triple[:, :, 0].astype(jnp.float32), axis=(0, 1))
    bias_self_v = jnp.sum(grad_triple[:, :, 2].astype(jnp.float32), axis=(0, 1))
    grad_self_in = join_back(
        jnp.einsum("cnkw,kwd->cnd", grad_triple, self_qkv, preferred_element_type=jnp.float32)
    )
    unused, norm_pull = jax.vjp(normed, after_mlp, norm_gain[3], norm_bias[3])
    grad_ln_three, gain_three, shift_three = norm_pull(grad_self_in)
    grad_state = grad_state + grad_ln_three
    bias_cross_mlp = jnp.sum(grad_state, axis=(0, 1))
    grad_ln_two, grad_cross_up, upbias_cross, grad_cross_down, gain_two, shift_two = feed_back(
        after_cross, norm_gain[2], norm_bias[2], cross_up, cross_down, cross_saved, grad_state
    )
    grad_state = grad_state + grad_ln_two
    bias_cross_attn = jnp.sum(grad_state, axis=(0, 1))
    grad_attn_in = grad_state.astype(jnp.bfloat16)
    grad_cross_out = jnp.einsum(
        "cnw,cnd->wd", cross_flat, grad_attn_in, preferred_element_type=jnp.float32
    )
    grad_mix = jnp.einsum(
        "cnd,wd->cnw", grad_attn_in, cross_out, preferred_element_type=jnp.float32
    ).astype(jnp.bfloat16)
    cross_grads = lax.map(
        back_parts, cross_parts + (cross_max, cross_totals, split_heads(grad_mix, heads_here))
    )
    grad_query_cross = (merge_heads(cross_grads[0]).astype(jnp.float32) * scaling).astype(
        jnp.bfloat16
    )
    grad_cross_q = jnp.einsum(
        "cnd,cnw->wd", latent_norm, grad_query_cross, preferred_element_type=jnp.float32
    )
    bias_cross_q = jnp.sum(grad_query_cross.astype(jnp.float32), axis=(0, 1))
    grad_latent_in = join_back(
        jnp.einsum("cnw,wd->cnd", grad_query_cross, cross_q, preferred_element_type=jnp.float32)
    )
    unused_too, latent_pull = jax.vjp(normed, start_state, norm_gain[1], norm_bias[1])
    grad_ln_one, gain_one, shift_one = latent_pull(grad_latent_in)
    grad_latents = grad_state + grad_ln_one
    grad_pair = jnp.stack([merge_heads(cross_grads[1]), merge_heads(cross_grads[2])], axis=2)
    grad_cross_kv = jnp.einsum(
        "cld,clkw->kwd", inputs, grad_pair, preferred_element_type=jnp.float32
    )
    bias_cross_v = jnp.sum(grad_pair[:, :, 1].astype(jnp.float32), axis=(0, 1))
    arrived = lax.all_to_all(grad_pair, "head", split_axis=1, concat_axis=3, tiled=True)
    grad_share = jnp.einsum(
        "clkw,kwd->cld", arrived, weights_whole, preferred_element_type=jnp.float32
    )
    own_start = head_index * rows_here
    own_mean = lax.dynamic_slice_in_dim(row_mean, own_start, rows_here, 1)
    own_inverse = lax.dynamic_slice_in_dim(inverse, own_start, rows_here, 1)
    standard = (tokens.astype(jnp.float32) - own_mean) * own_inverse
    scaled = grad_share * norm_gain[0]
    mean_plain = jnp.mean(scaled, axis=-1, keepdims=True)
    mean_cross = jnp.mean(scaled * standard, axis=-1, keepdims=True)
    grad_tokens = (own_inverse * (scaled - mean_plain - standard * mean_cross)).astype(jnp.bfloat16)
    gain_zero, shift_zero = lax.psum(
        (jnp.sum(grad_share * standard, axis=(0, 1)), jnp.sum(grad_share, axis=(0, 1))), "head"
    )
    grad_head_bias = jnp.stack(
        [jnp.stack([bias_cross_q, bias_cross_v]), jnp.stack([bias_self_q, bias_self_v])]
    )
    grad_up_bias = jnp.stack([upbias_cross, upbias_self])
    out_full = jnp.stack(
        [jnp.stack([bias_cross_attn, bias_cross_mlp]), jnp.stack([bias_self_attn, bias_self_mlp])]
    )
    grad_out_bias = share_of(out_full, head_index, head_width)
    grad_norm_gain = share_of(
        jnp.stack([gain_zero, gain_one, gain_two, gain_three, gain_four]), head_index, head_width
    )
    grad_norm_bias = share_of(
        jnp.stack([shift_zero, shift_one, shift_two, shift_three, shift_four]),
        head_index,
        head_width,
    )
    small_sums = lax.psum(
        (grad_head_bias, grad_up_bias, grad_out_bias, grad_norm_gain, grad_norm_bias), "dp"
    )
    pieces = [
        grad_cross_q.T,
        grad_cross_kv[0].T,
        grad_cross_kv[1].T,
        grad_cross_out.T,
        grad_self_qkv[0].T,
        grad_self_qkv[1].T,
        grad_self_qkv[2].T,
        grad_self_out.T,
        grad_cross_up,
        grad_cross_down.T,
        grad_self_up,
        grad_self_down.T,
    ]
    packed = jnp.concatenate([piece.astype(jnp.bfloat16) for piece in pieces], axis=1)
    summed = lax.psum_scatter(packed, "dp", scatter_dimension=0, tiled=True).astype(jnp.float32)
    sums = []
    start = 0
    for piece in pieces:
        sums.append(summed[:, start : start + piece.shape[1]])
        start += piece.shape[1]
    return (
        latents_out,
        grad_tokens,
        grad_latents,
        sums[0].T,
        jnp.stack([sums[1].T, sums[2].T]),
        sums[3].T,
        sums[8],
        sums[9].T,
        jnp.stack([sums[4].T, sums[5].T, sums[6].T]),
        sums[7].T,
        sums[10],
        sums[11].T,
        small_sums[0],
        small_sums[1],
        small_sums[2],
        small_sums[3],
        small_sums[4],
    )


def solution(mesh):
    in_specs = (
        P("dp", "head", None),
        P("dp"),
        P("dp", None),
        P("dp", None, None),
        P("head", None),
        P(None, "head", None),
        P("head", None),
        P(None, "head"),
        P("head", None),
        P(None, "head", None),
        P("head", None),
        P(None, "head"),
        P("head", None),
        P(None, None, "head"),
        P(None, "head"),
        P(),
        P(),
        P(),
        P("dp", None, None),
    )
    out_specs = (
        P("dp", None, None),
        P("dp", "head", None),
        P("dp", None, None),
        P("head", "dp"),
        P(None, "head", "dp"),
        P("head", "dp"),
        P("dp", "head"),
        P("head", "dp"),
        P(None, "head", "dp"),
        P("head", "dp"),
        P("dp", "head"),
        P("head", "dp"),
        P(None, None, "head"),
        P(None, "head"),
        P(None, None, "head"),
        P(None, "head"),
        P(None, "head"),
    )
    return jax.shard_map(local, mesh=mesh, in_specs=in_specs, out_specs=out_specs, check_vma=False)
```

profile of v0, /device:TPU:0, one launch (start us, length us, event | category | flops | bytes accessed | tf_op | source)
XLA Modules:
  0.0 712.1 jit_solution(15768888642467319990)
XLA Ops:
  7.3 18.4 %copy.67 = bf16[1,1578,768]{2,0,1:T(2,128)(2,1)} copy(bf16[1,1578,768]{2,1,0:T(8,128)(2,1)} %param.19) | data formatting | bytes 4847616 | tf_op args[0]
  28.8 122.7 %all-gather.3.cloned.1.call-done = bf16[1,6312,768]{2,0,1:T(2,128)(2,1)} async-done(((bf16[1,1578,768]{2,0,1:T(2,128)(2,1)}), bf16[1,6312,768]{2,0,1:T(2,128)(2,1)}) %all-gather.3.cloned.1.call-update) | async-done | bytes 9695248 | tf_op jit(solution)/shard_map/all_gather | solution.py:146
  151.5 7.5 %convert_reduce_fusion = f32[6312]{0:T(1024)S(1)} fusion(bf16[1,6312,768]{2,0,1:T(2,128)(2,1)} %all-gather.3.cloned.1.call-done), kind=kLoop, calls=%fused_computation.3 | loop fusion | flops 9688920 | bytes 9720480 | tf_op jit(solution)/shard_map/reduce_sum | solution.py:150
  159.0 14.1 %fusion.4 = f32[6312]{0:T(1024)S(1)} fusion(f32[6312]{0:T(1024)S(1)} %broadcast_multiply_fusion, bf16[1,6312,768]{2,0,1:T(2,128)(2,1)} %all-gather.3.cloned.1.call-done), kind=kLoop, calls=%fused_computation.6 | loop fusion | flops 19384152 | bytes 9745728 | tf_op jit(solution)/shard_map/reduce_sum | solution.py:152
  173.2 5.6 fusion.10
  178.9 4.1 convolution_bitcast_fusion
  185.2 3.1 convolution_select_fusion
  188.3 6.2 fusion.167
  194.6 5.0 fusion.45
  201.4 31.3 %all-reduce.12.cloned.1.call-done = bf16[1,128,768]{2,1,0:T(8,128)(2,1)} async-done(((bf16[1,128,768]{2,1,0:T(8,128)(2,1)}), bf16[1,128,768]{2,1,0:T(8,128)(2,1)}) %all-reduce.12.cloned.1.call-update) | async-done | bytes 196624 | tf_op jit(solution)/shard_map/psum | solution.py:36
  239.6 30.8 %all-reduce.14.cloned.1.call-done = bf16[1,128,768]{2,1,0:T(8,128)(2,1)} async-done(((bf16[1,128,768]{2,1,0:T(8,128)(2,1)}), bf16[1,128,768]{2,1,0:T(8,128)(2,1)}) %all-reduce.14.cloned.1.call-update) | async-done | bytes 196624 | tf_op jit(solution)/shard_map/psum | solution.py:36
  280.2 32.1 %all-reduce.16.cloned.1.call-done = bf16[1,128,768]{2,1,0:T(8,128)(2,1)} async-done(((bf16[1,128,768]{2,1,0:T(8,128)(2,1)}), bf16[1,128,768]{2,1,0:T(8,128)(2,1)}) %all-reduce.16.cloned.1.call-update) | async-done | bytes 196624 | tf_op jit(solution)/shard_map/psum | solution.py:36
  316.0 2.6 convert_reduce_fusion.7
  320.7 32.1 %all-reduce.18.cloned.1.call-done = bf16[1,128,768]{2,1,0:T(8,128)(2,1)} async-done(((bf16[1,128,768]{2,1,0:T(8,128)(2,1)}), bf16[1,128,768]{2,1,0:T(8,128)(2,1)}) %all-reduce.18.cloned.1.call-update) | async-done | bytes 196624 | tf_op jit(solution)/shard_map/psum | solution.py:40
  369.1 32.1 %all-reduce.20.cloned.1.call-done = bf16[1,128,768]{2,1,0:T(8,128)(2,1)} async-done(((bf16[1,128,768]{2,1,0:T(8,128)(2,1)}), bf16[1,128,768]{2,1,0:T(8,128)(2,1)}) %all-reduce.20.cloned.1.call-update) | async-done | bytes 196624 | tf_op jit(solution)/shard_map/psum | solution.py:40
  409.8 2.4 fusion.40
  412.3 29.7 %all-reduce.22.cloned.1.call-done = bf16[1,128,768]{2,1,0:T(8,128)(2,1)} async-done(((bf16[1,128,768]{2,1,0:T(8,128)(2,1)}), bf16[1,128,768]{2,1,0:T(8,128)(2,1)}) %all-reduce.22.cloned.1.call-update) | async-done | bytes 196624 | tf_op jit(solution)/shard_map/psum | solution.py:40
  449.2 11.8 %multiply_reduce_fusion = (f32[3,128]{1,0:T(4,128)S(1)}, f32[3,128,6312]{1,2,0:T(8,128)}) fusion(f32[3,128,6312]{1,2,0:T(8,128)} %get-tuple-element.268, f32[3,128]{1,0:T(4,128)S(1)} %copy-done.87, bf16[128,3,64]{0,2,1:T(8,128)(2,1)S(1)} %bitcast.305, f32[6312,3,64]{0,2,1:T(8,128)} %bitcast.281, f32[3,64]{1,0:T(4,128)S(1)} %copy-done.98), kind=kOutput, calls=%fused_computation.16 | convolution fusion | flops 319942272 | bytes 24291072 | tf_op jit(solution)/shard_map/while/body/eval_jaxpr/qhe,khe->hqk/dot_general | solution.py:67
  461.0 9.9 %multiply_convert_fusion = bf16[3,128,6312]{1,2,0:T(8,128)(2,1)} fusion(f32[3,128,6312]{1,2,0:T(8,128)} %get-tuple-element.274, f32[3,128]{1,0:T(4,128)S(1)} %get-tuple-element.273, f32[3,128,6312]{1,2,0:T(8,128)} %get-tuple-element.268, f32[3,128]{1,0:T(4,128)S(1)} %copy-done.87), kind=kLoop, calls=%fused_computation.15 | loop fusion | flops 9695232 | bytes 24241152 | tf_op jit(solution)/shard_map/while/body/eval_jaxpr/convert_element_type | solution.py:69
  470.9 4.9 convert_reduce_fusion.11
  478.5 6.3 convert_reduce_fusion.1
  487.9 7.9 %fusion.26 = bf16[2,192,768]{2,1,0:T(8,128)(2,1)S(1)} fusion(bf16[6312,768,1]{1,0,2:T(8,128)(2,1)} %copy-done.8, bf16[1,6312,1,192]{1,3,2,0:T(8,128)(2,1)S(1)} %bitcast.282, bf16[1,6312,1,192]{1,3,2,0:T(8,128)(2,1)S(1)} %bitcast.277), kind=kOutput, calls=%fused_computation.50 | convolution fusion | flops 3725687808 | bytes 15132672 | tf_op jit(solution)/shard_map/cld,clkw->kwd/dot_general | solution.py:273
  507.9 10.3 %copy.85 = bf16[768,4608]{1,0:T(8,128)(2,1)} copy(bf16[768,4608]{0,1:T(8,128)(2,1)} %fusion.25) | data formatting | bytes 14155776
  518.2 5.6 pad_maximum_fusion
  523.8 16.4 %copy.73 = bf16[1,6312,2,192]{3,2,0,1:T(2,128)(2,1)} copy(bf16[1,6312,2,192]{1,3,2,0:T(8,128)(2,1)} %pad_maximum_fusion) | data formatting | bytes 9695232 | tf_op jit(solution)/shard_map/stack | solution.py:272
  540.4 5.5 all-to-all-start
  552.7 65.7 %all-to-all-done = bf16[1,6312,2,192]{3,2,0,1:T(2,128)(2,1)} async-done(((bf16[1,6312,2,192]{3,2,0,1:T(2,128)(2,1)}), bf16[1,6312,2,192]{3,2,0,1:T(2,128)(2,1)}, u32[]{:S(2)}, u32[]{:S(2)}) %all-to-all-start) | async-done | bytes 4847648 | tf_op jit(solution)/shard_map/all_to_all | solution.py:277
  618.4 17.0 %copy.74 = bf16[1,4,1578,2,192]{2,4,1,3,0:T(8,128)(2,1)} copy(bf16[1,4,1578,2,192]{4,3,2,1,0:T(2,128)(2,1)} %bitcast.46) | data formatting | bytes 9695232 | tf_op jit(solution)/shard_map/all_to_all | solution.py:277
  635.4 9.5 %fusion.13 = (f32[768]{0:T(1024)S(1)}, f32[1578]{0:T(1024)S(1)}, f32[1578,768,1]{1,0,2:T(8,128)S(1)}) fusion(bf16[1,1578,768]{2,1,0:T(8,128)(2,1)} %param.19, f32[1578]{0:T(1024)S(1)} %dynamic_slice.65, f32[1578]{0:T(1024)S(1)} %dynamic_slice.64, f32[768]{0:T(1024)S(1)} %copy-done.44, bf16[1578,2,768]{0,2,1:T(8,128)(2,1)} %bitcast.279, ...), kind=kOutput, calls=%fused_computation.26 | convolution fusion | flops 3732662016 | bytes 14503416 | tf_op jit(solution)/shard_map/clkw,kwd->cld/dot_general | solution.py:278
  647.8 6.2 all-reduce.2
  654.1 38.3 %all-reduce.1 = (f32[2,2,192]{2,1,0:T(2,128)}, f32[2,768]{1,0:T(2,128)}, f32[2,2,192]{2,1,0:T(2,128)}, f32[5,192]{1,0:T(8,128)}, f32[5,192]{1,0:T(8,128)}) all-reduce(f32[2,2,192]{2,1,0:T(2,128)S(1)} %pad_maximum_fusion.4, f32[2,768]{1,0:T(2,128)S(1)} %pad_maximum_fusion.3, ...), channel_id=1, replica_groups=mesh['dp'=8,'head'=4] {'dp'}, use_global_device_ids=true, to_apply=%region_39.40 | all-reduce | flops 4992 | bytes 39936 | tf_op jit(solution)/shard_map/psum | solution.py:308
  692.5 5.0 fusion.16
  (374 shorter events, 95.3 us)
Async XLA Ops:
  7.2 230.0 %copy-start = (bf16[768,768]{1,0:T(8,128)(2,1)S(1)}, bf16[768,768]{1,0:T(8,128)(2,1)}, u32[]{:S(2)}) copy-start(bf16[768,768]{1,0:T(8,128)(2,1)} %param.27) | copy-start | bytes 3538948
  7.3 144.2 %all-gather.3.cloned.1.call-start = ((), (), s32[]{:S(2)}) async-start(), calls=%async_computation.2 | async-start | bytes 24238080 | tf_op jit(solution)/shard_map/all_gather | solution.py:146
  25.7 207.0 %all-reduce.12.cloned.1.call-start = ((), (), s32[]{:S(2)}) async-start(), calls=%async_computation.3 | async-start | bytes 393216 | tf_op jit(solution)/shard_map/psum | solution.py:36
  25.9 168.6 %copy-start.97 = (f32[3,64]{1,0:T(4,128)}, f32[3,64]{1,0:T(4,128)S(1)}, u32[]{:S(2)}) copy-start(f32[3,64]{1,0:T(4,128)S(1)} %add.328) | copy-start | bytes 2308
  27.9 131.0 %copy-start.89 = (f32[768]{0:T(1024)}, f32[768]{0:T(1024)S(1)}, u32[]{:S(2)}) copy-start(f32[768]{0:T(1024)S(1)} %get-tuple-element.220) | copy-start | bytes 9220
  27.9 207.1 %copy-start.48 = (f32[768]{0:T(1024)}, f32[768]{0:T(1024)S(1)}, u32[]{:S(2)}) copy-start(f32[768]{0:T(1024)S(1)} %get-tuple-element.219) | copy-start | bytes 9220
  28.0 130.9 %copy-start.45 = (f32[768]{0:T(1024)}, f32[768]{0:T(1024)S(1)}, u32[]{:S(2)}) copy-start(f32[768]{0:T(1024)S(1)} %get-tuple-element.215) | copy-start | bytes 9220
  28.0 145.1 %copy-start.43 = (f32[768]{0:T(1024)}, f32[768]{0:T(1024)S(1)}, u32[]{:S(2)}) copy-start(f32[768]{0:T(1024)S(1)} %get-tuple-element.216) | copy-start | bytes 9220
  28.1 130.8 %copy-start.77 = (f32[128]{0:T(128)}, f32[128]{0:T(128)S(1)}, u32[]{:S(2)}) copy-start(f32[128]{0:T(128)S(1)} %broadcast_multiply_fusion.6) | copy-start | bytes 1540
  28.4 130.6 %copy-start.101 = (f32[128]{0:T(128)}, f32[128]{0:T(128)S(1)}, u32[]{:S(2)}) copy-start(f32[128]{0:T(128)S(1)} %fusion.86) | copy-start | bytes 1540
  28.4 130.6 %copy-start.94 = (f32[128]{0:T(128)}, f32[128]{0:T(128)S(1)}, u32[]{:S(2)}) copy-start(f32[128]{0:T(128)S(1)} %fusion.133) | copy-start | bytes 1540
  28.7 154.8 %copy-start.35 = (bf16[128,192]{0,1:T(8,128)(2,1)}, bf16[128,192]{0,1:T(8,128)(2,1)S(1)}, u32[]{:S(2)}) copy-start(bf16[128,192]{0,1:T(8,128)(2,1)S(1)} %fusion.44) | copy-start | bytes 147460
  199.6 70.8 %copy-start.39 = (bf16[3,64,128]{2,1,0:T(8,128)(2,1)}, bf16[3,64,128]{2,1,0:T(8,128)(2,1)S(1)}, u32[]{:S(2)}) copy-start(bf16[3,64,128]{2,1,0:T(8,128)(2,1)S(1)} %fusion.45) | copy-start | bytes 147460
  199.6 70.8 %copy-start.60 = (f32[768]{0:T(1024)S(1)}, f32[768]{0:T(1024)}, u32[]{:S(2)}) copy-start(f32[768]{0:T(1024)} %get-tuple-element.224) | copy-start | bytes 9220
  199.6 72.2 %copy-start.50 = (f32[768]{0:T(1024)S(1)}, f32[768]{0:T(1024)}, u32[]{:S(2)}) copy-start(f32[768]{0:T(1024)} %get-tuple-element.222) | copy-start | bytes 9220
  200.6 69.8 %all-reduce.14.cloned.1.call-start = ((), (), s32[]{:S(2)}) async-start(), calls=%async_computation.4 | async-start | bytes 393216 | tf_op jit(solution)/shard_map/psum | solution.py:36
  201.4 77.0 %copy-start.19 = (bf16[192,768]{1,0:T(8,128)(2,1)S(1)}, bf16[192,768]{1,0:T(8,128)(2,1)}, u32[]{:S(2)}) copy-start(bf16[192,768]{1,0:T(8,128)(2,1)} %param.29) | copy-start | bytes 884740
  237.1 77.1 %copy-start.10 = (bf16[768,768]{1,0:T(8,128)(2,1)S(1)}, bf16[768,768]{1,0:T(8,128)(2,1)}, u32[]{:S(2)}) copy-start(bf16[768,768]{1,0:T(8,128)(2,1)} %param.30) | copy-start | bytes 3538948
  238.2 74.1 %all-reduce.16.cloned.1.call-start = ((), (), s32[]{:S(2)}) async-start(), calls=%async_computation.5 | async-start | bytes 393216 | tf_op jit(solution)/shard_map/psum | solution.py:36
  280.1 72.6 %all-reduce.18.cloned.1.call-start = ((), (), s32[]{:S(2)}) async-start(), calls=%async_computation.6 | async-start | bytes 393216 | tf_op jit(solution)/shard_map/psum | solution.py:40
  320.6 82.5 %copy-start.105 = (f32[128]{0:T(128)S(1)}, f32[128]{0:T(128)}, u32[]{:S(2)}) copy-start(f32[128]{0:T(128)} %copy-done.104) | copy-start | bytes 1540
  320.6 82.5 %copy-start.53 = (f32[128]{0:T(128)S(1)}, f32[128]{0:T(128)}, u32[]{:S(2)}) copy-start(f32[128]{0:T(128)} %copy-done.52) | copy-start | bytes 1540
  320.6 82.5 %copy-start.75 = (f32[128]{0:T(128)S(1)}, f32[128]{0:T(128)}, u32[]{:S(2)}) copy-start(f32[128]{0:T(128)} %copy-done.74) | copy-start | bytes 1540
  320.6 86.1 %copy-start.15 = (f32[128,768]{1,0:T(8,128)S(1)}, f32[128,768]{1,0:T(8,128)}, u32[]{:S(2)}) copy-start(f32[128,768]{1,0:T(8,128)} %copy-done.14) | copy-start | bytes 1179652
  320.6 80.6 %all-reduce.20.cloned.1.call-start = ((), (), s32[]{:S(2)}) async-start(), calls=%async_computation.7 | async-start | bytes 393216 | tf_op jit(solution)/shard_map/psum | solution.py:40
  361.9 43.0 %copy-start.37 = (bf16[3,64,128]{2,1,0:T(8,128)(2,1)}, bf16[3,64,128]{2,1,0:T(8,128)(2,1)S(1)}, u32[]{:S(2)}) copy-start(bf16[3,64,128]{2,1,0:T(8,128)(2,1)S(1)} %get-tuple-element.277) | copy-start | bytes 147460
  369.1 72.9 %all-reduce.22.cloned.1.call-start = ((), (), s32[]{:S(2)}) async-start(), calls=%async_computation.8 | async-start | bytes 393216 | tf_op jit(solution)/shard_map/psum | solution.py:40
  407.9 41.3 %copy-start.98 = (f32[3,64]{1,0:T(4,128)S(1)}, f32[3,64]{1,0:T(4,128)}, u32[]{:S(2)}) copy-start(f32[3,64]{1,0:T(4,128)} %copy-done.97) | copy-start | bytes 2308
  409.8 138.4 %all-reduce.24.cloned.1.call-start = ((), (), s32[]{:S(2)}) async-start(), calls=%async_computation.11 | async-start | bytes 786432 | tf_op jit(solution)/shard_map/psum | solution.py:36
  476.8 158.6 %all-gather.5.cloned.1.call-start = ((), (), s32[]{:S(2)}) async-start(), calls=%async_computation.9 | async-start | bytes 2949120 | tf_op jit(solution)/shard_map/all_gather | solution.py:147
  477.5 220.0 %reduce-scatter.4.cloned.1.call-start = ((), (), s32[]{:S(2)}) async-start(), calls=%async_computation.10 | async-start | bytes 7962624
  540.4 78.0 %all-to-all-start = ((bf16[1,6312,2,192]{3,2,0,1:T(2,128)(2,1)}), bf16[1,6312,2,192]{3,2,0,1:T(2,128)(2,1)}, u32[]{:S(2)}, u32[]{:S(2)}) async-start(bf16[1,6312,2,192]{3,2,0,1:T(2,128)(2,1)} %copy.73), calls=%async_computation | async-start | bytes 12926976 | tf_op jit(solution)/shard_map/all_to_all | solution.py:277
  (89 other events, 1018.3 us)
Sparse Core Ops, SparseCore 0:
  25.9 125.5 all-gather.2
  200.7 32.0 all-reduce.11
  238.3 32.0 all-reduce.13
  280.3 32.0 all-reduce.15
  320.7 31.9 all-reduce.17
  369.2 32.0 all-reduce.19
  409.9 32.0 all-reduce.21
  476.9 32.9 all-reduce.23
  511.4 24.0 all-gather.4
  539.0 129.7 reduce-scatter.3
where the time goes:
time: 720 us; the launch traced here: 712 us
  waiting for transfers between devices  377 us (52%)
  matrix products  95.7 us (13%)
  local copies, waits for them, and re-layouts  86.2 us (12%)
  other arithmetic  85.1 us (12%)
  blocking collectives  44.6 us (6%)
  between operations  16.6 us (2%)
    all_gather x1, waiting for transfers between devices, local(): lax.all_gather(tokens, 'head', axis=1, tiled=True)  123 us
    psum x4, waiting for transfers between devices, join_heads(): lax.psum(partial_sum.astype(jnp.bfloat16), 'head').astype(jnp.float32)  94.3 us
    psum x3, waiting for transfers between devices, join_back(): lax.psum(partial_sum.astype(jnp.bfloat16), 'head').astype(jnp.float32)  93.9 us
    all_to_all x1, waiting for transfers between devices, local(): lax.all_to_all(grad_pair, 'head', split_axis=1, concat_axis=3, tiled=True)  65.7 us
    unnamed x232, local copies, waits for them, and re-layouts  45.2 us
    psum x1, blocking collectives, local(): lax.psum((grad_head_bias, grad_up_bias, grad_out_bias, grad_norm_gain, gr...  38.3 us
    all_to_all x1, local copies, waits for them, and re-layouts, local(): lax.all_to_all(grad_pair, 'head', split_axis=1, concat_axis=3, tiled=True)  17 us
    another operation x1, local copies, waits for them, and re-layouts, local(): jnp.stack([merge_heads(cross_grads[1]), merge_heads(cross_grads[2])], axi...  16.4 us
  transfers between devices with their start and end apart: 11, of which 8 were waited for; matrix products, arithmetic and copies ran while one was open for 15% of the time, Pallas kernels for 0%

commit v1 on v0

--- a/solution.py
+++ b/solution.py
@@ -9,6 +9,22 @@
 F_MAX = 16
 EPSILON = 1e-05
 NEGATIVE = -1e30
+
+
+def ring_gather(x, axis, dim):
+    ways, here, step = (lax.axis_size(axis), lax.axis_index(axis), x.shape[dim])
+    dims = [n * ways if d == dim else n for d, n in enumerate(x.shape)]
+    full = lax.dynamic_update_slice_in_dim(jnp.zeros(dims, x.dtype), x, here * step, axis=dim)
+    going_up = going_down = x
+    for far in range(1, ways // 2 + 1):
+        going_up = lax.ppermute(going_up, axis, [(d, (d + 1) % ways) for d in range(ways)])
+        full = lax.dynamic_update_slice_in_dim(full, going_up, (here - far) % ways * step, axis=dim)
+        if 2 * far < ways:
+            going_down = lax.ppermute(going_down, axis, [(d, (d - 1) % ways) for d in range(ways)])
+            full = lax.dynamic_update_slice_in_dim(
+                full, going_down, (here + far) % ways * step, axis=dim
+            )
+    return full
 
 
 def normed(tensor, gain_row, shift_row):
@@ -143,7 +159,7 @@
     )
     usable = (position[None, :] < frames[:, None] * P_SIZE) | (text_full == 1)
     gathered, weights_whole = (
-        lax.all_gather(tokens, "head", axis=1, tiled=True),
+        ring_gather(tokens, "head", 1),
         lax.all_gather(cross_kv, "head", axis=1, tiled=True),
     )
     full_rows = gathered.astype(jnp.float32)

time: 720 us -> 672 us (0.933)
  waiting for transfers between devices: 377 us -> 310 us
  local copies, waits for them, and re-layouts: 86.2 us -> 121 us
  other arithmetic: 85.1 us -> 68.3 us
    all_gather x1 -> x0, waiting for transfers between devices: 123 us -> none  [local(): lax.all_gather(tokens, 'head', axis=1, tiled=True)]
    ppermute x0 -> x3, waiting for transfers between devices: none -> 51 us  [the longest x2 51 us: ring_gather(): lax.ppermute(going_up, axis, [(d, (d + 1) % ways) for d in range(ways)])]
    dynamic_update_slice x0 -> x4, local copies, waits for them, and re-layouts: none -> 49.9 us  [the longest x2 24.7 us: ring_gather(): lax.dynamic_update_slice_in_dim(full, going_up, (here - far) % ways * ste...]
    unnamed x232 -> x261, local copies, waits for them, and re-layouts: 45.2 us -> 26.8 us
    reduce_sum x1, other arithmetic: 14.1 us -> 5.23 us  [local(): jnp.mean(centered * centered, axis=-1, keepdims=True) + EPSILON]
  transfers between devices with their start and end apart: 11 -> 13, of which waited for: 8 -> 8; matrix products, arithmetic and copies ran while one was open for 15% -> 22% of each run, Pallas kernels for 0% -> 0%
where the time goes in v1:
time: 672 us; the launch traced here: 665 us
  waiting for transfers between devices  310 us (46%)
  local copies, waits for them, and re-layouts  121 us (18%)
  matrix products  93.6 us (14%)
  other arithmetic  68.3 us (10%)
  blocking collectives  44.3 us (7%)
  between operations  16.5 us (2%)
  starting transfers between devices  11.2 us (2%)
    psum x4, waiting for transfers between devices, join_heads(): lax.psum(partial_sum.astype(jnp.bfloat16), 'head').astype(jnp.float32)  97.5 us
    psum x3, waiting for transfers between devices, join_back(): lax.psum(partial_sum.astype(jnp.bfloat16), 'head').astype(jnp.float32)  93.9 us
    all_to_all x1, waiting for transfers between devices, local(): lax.all_to_all(grad_pair, 'head', split_axis=1, concat_axis=3, tiled=True)  67 us
    ppermute x2, waiting for transfers between devices, ring_gather(): lax.ppermute(going_up, axis, [(d, (d + 1) % ways) for d in range(ways)])  51 us
    psum x1, blocking collectives, local(): lax.psum((grad_head_bias, grad_up_bias, grad_out_bias, grad_norm_gain, gr...  38.2 us
    unnamed x261, local copies, waits for them, and re-layouts  26.8 us
    dynamic_update_slice x2, local copies, waits for them, and re-layouts, ring_gather(): lax.dynamic_update_slice_in_dim(full, going_up, (here - far) % ways * ste...  24.7 us
    all_to_all x1, local copies, waits for them, and re-layouts, local(): lax.all_to_all(grad_pair, 'head', split_axis=1, concat_axis=3, tiled=True)  17 us
  transfers between devices with their start and end apart: 13, of which 8 were waited for; matrix products, arithmetic and copies ran while one was open for 22% of the time, Pallas kernels for 0%

profile of v1, /device:TPU:0, one launch (start us, length us, event | category | flops | bytes accessed | tf_op | source)
XLA Modules:
  0.0 664.8 jit_solution(2277514992694341858)
XLA Ops:
  9.8 51.0 %collective-permute-done = bf16[1,1578,768]{2,1,0:T(8,128)(2,1)} collective-permute-done((bf16[1,1578,768]{2,1,0:T(8,128)(2,1)}, bf16[1,1578,768]{2,1,0:T(8,128)(2,1)}, u32[]{:S(2)}, u32[]{:S(2)}) %collective-permute-start) | collective-permute-done | bytes 2423840 | tf_op jit(solution)/shard_map/ppermute | solution.py:20
  64.8 4.3 broadcast_in_dim.155
  69.2 12.7 %dynamic_update_slice.39 = bf16[1,6312,768]{2,1,0:T(8,128)(2,1)} dynamic-update-slice(bf16[1,6312,768]{2,1,0:T(8,128)(2,1)} %broadcast_in_dim.155, bf16[1,1578,768]{2,1,0:T(8,128)(2,1)} %param.19, s32[]{:T(128)} %constant.158.clone.1, s32[]{:T(128)S(6)} %select_n.46, s32[]{:T(128)} %constant.158.clone.1) | dynamic-update-slice | bytes 4847620 | tf_op jit(solution)/shard_map/dynamic_update_slice | solution.py:17
  83.5 12.1 %dynamic_update_slice.40 = bf16[1,6312,768]{2,1,0:T(8,128)(2,1)} dynamic-update-slice(bf16[1,6312,768]{2,1,0:T(8,128)(2,1)} %dynamic_update_slice.39, bf16[1,1578,768]{2,1,0:T(8,128)(2,1)} %collective-permute-done, s32[]{:T(128)} %constant.158.clone.1, s32[]{:T(128)S(6)} %select_n.48, s32[]{:T(128)} %constant.158.clone.1) | dynamic-update-slice | bytes 4847620 | tf_op jit(solution)/shard_map/dynamic_update_slice | solution.py:21
  95.6 12.6 %dynamic_update_slice.41 = bf16[1,6312,768]{2,1,0:T(8,128)(2,1)} dynamic-update-slice(bf16[1,6312,768]{2,1,0:T(8,128)(2,1)} %dynamic_update_slice.40, bf16[1,1578,768]{2,1,0:T(8,128)(2,1)} %collective-permute-done.1, s32[]{:T(128)} %constant.158.clone.1, s32[]{:T(128)S(6)} %select_n.50, s32[]{:T(128)} %constant.158.clone.1) | dynamic-update-slice | bytes 4847620 | tf_op jit(solution)/shard_map/dynamic_update_slice | solution.py:24
  108.2 12.6 %dynamic_update_slice.42 = bf16[1,6312,768]{2,1,0:T(8,128)(2,1)} dynamic-update-slice(bf16[1,6312,768]{2,1,0:T(8,128)(2,1)} %dynamic_update_slice.41, bf16[1,1578,768]{2,1,0:T(8,128)(2,1)} %collective-permute-done.2, s32[]{:T(128)} %constant.158.clone.1, s32[]{:T(128)S(6)} %select_n.52, s32[]{:T(128)} %constant.158.clone.1) | dynamic-update-slice | bytes 4847620 | tf_op jit(solution)/shard_map/dynamic_update_slice | solution.py:21
  120.8 5.3 convert_reduce_fusion
  127.3 5.2 fusion.4
  132.6 4.7 convolution_bitcast_fusion
  143.1 6.3 fusion.169
  149.4 6.4 fusion.45
  157.4 33.4 %all-reduce.12.cloned.1.call-done = bf16[1,128,768]{2,1,0:T(8,128)(2,1)} async-done(((bf16[1,128,768]{2,1,0:T(8,128)(2,1)}), bf16[1,128,768]{2,1,0:T(8,128)(2,1)}) %all-reduce.12.cloned.1.call-update) | async-done | bytes 196624 | tf_op jit(solution)/shard_map/psum | solution.py:52
  196.9 32.0 %all-reduce.14.cloned.1.call-done = bf16[1,128,768]{2,1,0:T(8,128)(2,1)} async-done(((bf16[1,128,768]{2,1,0:T(8,128)(2,1)}), bf16[1,128,768]{2,1,0:T(8,128)(2,1)}) %all-reduce.14.cloned.1.call-update) | async-done | bytes 196624 | tf_op jit(solution)/shard_map/psum | solution.py:52
  233.3 32.1 %all-reduce.16.cloned.1.call-done = bf16[1,128,768]{2,1,0:T(8,128)(2,1)} async-done(((bf16[1,128,768]{2,1,0:T(8,128)(2,1)}), bf16[1,128,768]{2,1,0:T(8,128)(2,1)}) %all-reduce.16.cloned.1.call-update) | async-done | bytes 196624 | tf_op jit(solution)/shard_map/psum | solution.py:52
  275.0 32.1 %all-reduce.18.cloned.1.call-done = bf16[1,128,768]{2,1,0:T(8,128)(2,1)} async-done(((bf16[1,128,768]{2,1,0:T(8,128)(2,1)}), bf16[1,128,768]{2,1,0:T(8,128)(2,1)}) %all-reduce.18.cloned.1.call-update) | async-done | bytes 196624 | tf_op jit(solution)/shard_map/psum | solution.py:56
  322.5 32.1 %all-reduce.20.cloned.1.call-done = bf16[1,128,768]{2,1,0:T(8,128)(2,1)} async-done(((bf16[1,128,768]{2,1,0:T(8,128)(2,1)}), bf16[1,128,768]{2,1,0:T(8,128)(2,1)}) %all-reduce.20.cloned.1.call-update) | async-done | bytes 196624 | tf_op jit(solution)/shard_map/psum | solution.py:56
  367.4 29.7 %all-reduce.22.cloned.1.call-done = bf16[1,128,768]{2,1,0:T(8,128)(2,1)} async-done(((bf16[1,128,768]{2,1,0:T(8,128)(2,1)}), bf16[1,128,768]{2,1,0:T(8,128)(2,1)}) %all-reduce.22.cloned.1.call-update) | async-done | bytes 196624 | tf_op jit(solution)/shard_map/psum | solution.py:56
  403.3 11.8 %multiply_reduce_fusion = (f32[3,128]{1,0:T(4,128)S(1)}, f32[3,128,6312]{1,2,0:T(8,128)}) fusion(f32[3,128,6312]{1,2,0:T(8,128)} %get-tuple-element.251, f32[3,128]{1,0:T(4,128)S(1)} %copy-done.99, bf16[128,3,64]{0,2,1:T(8,128)(2,1)S(1)} %bitcast.307, f32[6312,3,64]{0,2,1:T(8,128)} %bitcast.283, f32[3,64]{1,0:T(4,128)S(1)} %copy-done.111), kind=kOutput, calls=%fused_computation.16 | convolution fusion | flops 319942272 | bytes 24291072 | tf_op jit(solution)/shard_map/while/body/eval_jaxpr/qhe,khe->hqk/dot_general | solution.py:83
  415.1 9.9 %multiply_convert_fusion = bf16[3,128,6312]{1,2,0:T(8,128)(2,1)} fusion(f32[3,128,6312]{1,2,0:T(8,128)} %get-tuple-element.257, f32[3,128]{1,0:T(4,128)S(1)} %get-tuple-element.256, f32[3,128,6312]{1,2,0:T(8,128)} %get-tuple-element.251, f32[3,128]{1,0:T(4,128)S(1)} %copy-done.99), kind=kLoop, calls=%fused_computation.15 | loop fusion | flops 9695232 | bytes 24241152 | tf_op jit(solution)/shard_map/while/body/eval_jaxpr/convert_element_type | solution.py:85
  425.1 5.0 convert_reduce_fusion.11
  432.6 5.7 convert_reduce_fusion.1
  440.9 6.6 fusion.26
  460.9 10.5 %copy.71 = bf16[768,4608]{1,0:T(8,128)(2,1)} copy(bf16[768,4608]{0,1:T(8,128)(2,1)} %fusion.25) | data formatting | bytes 14155776
  471.4 5.5 pad_maximum_fusion
  477.0 16.4 %copy.59 = bf16[1,6312,2,192]{3,2,0,1:T(2,128)(2,1)} copy(bf16[1,6312,2,192]{1,3,2,0:T(8,128)(2,1)} %pad_maximum_fusion) | data formatting | bytes 9695232 | tf_op jit(solution)/shard_map/stack | solution.py:288
  493.6 5.3 all-to-all-start
  504.4 67.0 %all-to-all-done = bf16[1,6312,2,192]{3,2,0,1:T(2,128)(2,1)} async-done(((bf16[1,6312,2,192]{3,2,0,1:T(2,128)(2,1)}), bf16[1,6312,2,192]{3,2,0,1:T(2,128)(2,1)}, u32[]{:S(2)}, u32[]{:S(2)}) %all-to-all-start) | async-done | bytes 4847648 | tf_op jit(solution)/shard_map/all_to_all | solution.py:293
  571.4 17.0 %copy.60 = bf16[1,4,1578,2,192]{2,4,1,3,0:T(8,128)(2,1)} copy(bf16[1,4,1578,2,192]{4,3,2,1,0:T(2,128)(2,1)} %bitcast.46) | data formatting | bytes 9695232 | tf_op jit(solution)/shard_map/all_to_all | solution.py:293
  588.4 9.7 %fusion.13 = (f32[768]{0:T(1024)S(1)}, f32[1578]{0:T(1024)S(1)}, f32[1578,768,1]{1,0,2:T(8,128)S(1)}) fusion(bf16[1,1578,768]{2,1,0:T(8,128)(2,1)} %param.19, f32[1578]{0:T(1024)S(1)} %dynamic_slice.65, f32[1578]{0:T(1024)S(1)} %dynamic_slice.64, f32[768]{0:T(1024)S(1)} %copy-done.57, bf16[1578,2,768]{0,2,1:T(8,128)(2,1)} %bitcast.281, ...), kind=kOutput, calls=%fused_computation.26 | convolution fusion | flops 3732662016 | bytes 14503416 | tf_op jit(solution)/shard_map/clkw,kwd->cld/dot_general | solution.py:294
  601.0 6.1 all-reduce.2
  607.3 38.2 %all-reduce.1 = (f32[2,2,192]{2,1,0:T(2,128)}, f32[2,768]{1,0:T(2,128)}, f32[2,2,192]{2,1,0:T(2,128)}, f32[5,192]{1,0:T(8,128)}, f32[5,192]{1,0:T(8,128)}) all-reduce(f32[2,2,192]{2,1,0:T(2,128)S(1)} %pad_maximum_fusion.4, f32[2,768]{1,0:T(2,128)S(1)} %pad_maximum_fusion.3, ...), channel_id=1, replica_groups=mesh['dp'=8,'head'=4] {'dp'}, use_global_device_ids=true, to_apply=%region_39.40 | all-reduce | flops 4992 | bytes 39936 | tf_op jit(solution)/shard_map/psum | solution.py:324
  645.5 5.0 fusion.16
  (411 shorter events, 103.9 us)
Async XLA Ops:
  7.2 188.4 %copy-start = (bf16[768,768]{1,0:T(8,128)(2,1)S(1)}, bf16[768,768]{1,0:T(8,128)(2,1)}, u32[]{:S(2)}) copy-start(bf16[768,768]{1,0:T(8,128)(2,1)} %param.27) | copy-start | bytes 3538948
  7.2 183.5 %all-reduce.12.cloned.1.call-start = ((), (), s32[]{:S(2)}) async-start(), calls=%async_computation.2 | async-start | bytes 393216 | tf_op jit(solution)/shard_map/psum | solution.py:52
  7.3 53.6 %collective-permute-start = (bf16[1,1578,768]{2,1,0:T(8,128)(2,1)}, bf16[1,1578,768]{2,1,0:T(8,128)(2,1)}, u32[]{:S(2)}, u32[]{:S(2)}) collective-permute-start(bf16[1,1578,768]{2,1,0:T(8,128)(2,1)} %param.19), channel_id=1, source_target_pairs={{0,1},{1,2},{2,3},{3,0},{4,5},{5,6},{6,7},{7,4},{8,9},{9,10},{10,1... | collective-permute-start | bytes 7271432 | tf_op jit(solution)/shard_map/ppermute | solution.py:20
  7.8 87.8 %collective-permute-start.1 = (bf16[1,1578,768]{2,1,0:T(8,128)(2,1)}, bf16[1,1578,768]{2,1,0:T(8,128)(2,1)}, u32[]{:S(2)}, u32[]{:S(2)}) collective-permute-start(bf16[1,1578,768]{2,1,0:T(8,128)(2,1)} %param.19), channel_id=1, source_target_pairs={{0,3},{1,0},{2,1},{3,2},{4,7},{5,4},{6,5},{7,6},{8,11},{9,8},{10,9... | collective-permute-start | bytes 7271432 | tf_op jit(solution)/shard_map/ppermute | solution.py:23
  60.8 47.4 %collective-permute-start.2 = (bf16[1,1578,768]{2,1,0:T(8,128)(2,1)}, bf16[1,1578,768]{2,1,0:T(8,128)(2,1)}, u32[]{:S(2)}, u32[]{:S(2)}) collective-permute-start(bf16[1,1578,768]{2,1,0:T(8,128)(2,1)} %collective-permute-done), channel_id=1, source_target_pairs={{0,1},{1,2},{2,3},{3,0},{4,5},{5,6},{6,7},{7,4},{8,9},{9,10},{10,1... | collective-permute-start | bytes 7271432 | tf_op jit(solution)/shard_map/ppermute | solution.py:20
  64.1 85.3 %copy-start.110 = (f32[3,64]{1,0:T(4,128)}, f32[3,64]{1,0:T(4,128)S(1)}, u32[]{:S(2)}) copy-start(f32[3,64]{1,0:T(4,128)S(1)} %add.361) | copy-start | bytes 2308
  82.6 50.0 %copy-start.104 = (f32[768]{0:T(1024)}, f32[768]{0:T(1024)S(1)}, u32[]{:S(2)}) copy-start(f32[768]{0:T(1024)S(1)} %get-tuple-element.204) | copy-start | bytes 9220
  82.6 110.4 %copy-start.60 = (f32[768]{0:T(1024)}, f32[768]{0:T(1024)S(1)}, u32[]{:S(2)}) copy-start(f32[768]{0:T(1024)S(1)} %get-tuple-element.202) | copy-start | bytes 9220
  82.7 147.6 %copy-start.62 = (f32[768]{0:T(1024)}, f32[768]{0:T(1024)S(1)}, u32[]{:S(2)}) copy-start(f32[768]{0:T(1024)S(1)} %get-tuple-element.205) | copy-start | bytes 9220
  82.7 184.6 %copy-start.58 = (f32[768]{0:T(1024)}, f32[768]{0:T(1024)S(1)}, u32[]{:S(2)}) copy-start(f32[768]{0:T(1024)S(1)} %get-tuple-element.201) | copy-start | bytes 9220
  82.8 276.1 %copy-start.49 = (f32[768]{0:T(1024)}, f32[768]{0:T(1024)S(1)}, u32[]{:S(2)}) copy-start(f32[768]{0:T(1024)S(1)} %get-tuple-element.200) | copy-start | bytes 9220
  82.8 318.6 %copy-start.47 = (f32[768]{0:T(1024)}, f32[768]{0:T(1024)S(1)}, u32[]{:S(2)}) copy-start(f32[768]{0:T(1024)S(1)} %get-tuple-element.197) | copy-start | bytes 9220
  83.5 56.6 %copy-start.37 = (bf16[128,192]{0,1:T(8,128)(2,1)}, bf16[128,192]{0,1:T(8,128)(2,1)S(1)}, u32[]{:S(2)}) copy-start(bf16[128,192]{0,1:T(8,128)(2,1)S(1)} %fusion.44) | copy-start | bytes 147460
  155.9 76.4 %copy-start.43 = (bf16[3,64,128]{2,1,0:T(8,128)(2,1)}, bf16[3,64,128]{2,1,0:T(8,128)(2,1)S(1)}, u32[]{:S(2)}) copy-start(bf16[3,64,128]{2,1,0:T(8,128)(2,1)S(1)} %fusion.45) | copy-start | bytes 147460
  155.9 74.3 %copy-start.12 = (bf16[3,192,768]{2,1,0:T(8,128)(2,1)S(1)}, bf16[3,192,768]{2,1,0:T(8,128)(2,1)}, u32[]{:S(2)}) copy-start(bf16[3,192,768]{2,1,0:T(8,128)(2,1)} %param.28) | copy-start | bytes 2654212
  156.8 72.0 %all-reduce.14.cloned.1.call-start = ((), (), s32[]{:S(2)}) async-start(), calls=%async_computation.3 | async-start | bytes 393216 | tf_op jit(solution)/shard_map/psum | solution.py:52
  157.3 74.9 %copy-start.22 = (bf16[192,768]{1,0:T(8,128)(2,1)S(1)}, bf16[192,768]{1,0:T(8,128)(2,1)}, u32[]{:S(2)}) copy-start(bf16[192,768]{1,0:T(8,128)(2,1)} %param.29) | copy-start | bytes 884740
  191.9 209.4 %copy-start.66 = (f32[128]{0:T(128)}, f32[128]{0:T(128)S(1)}, u32[]{:S(2)}) copy-start(f32[128]{0:T(128)S(1)} %broadcast_multiply_fusion.5) | copy-start | bytes 1540
  196.7 68.7 %all-reduce.16.cloned.1.call-start = ((), (), s32[]{:S(2)}) async-start(), calls=%async_computation.4 | async-start | bytes 393216 | tf_op jit(solution)/shard_map/psum | solution.py:52
  196.8 69.7 %copy-start.113 = (f32[3,64]{1,0:T(4,128)}, f32[3,64]{1,0:T(4,128)S(1)}, u32[]{:S(2)}) copy-start(f32[3,64]{1,0:T(4,128)S(1)} %add.392) | copy-start | bytes 2308
  230.0 128.9 %copy-start.64 = (f32[128]{0:T(128)}, f32[128]{0:T(128)S(1)}, u32[]{:S(2)}) copy-start(f32[128]{0:T(128)S(1)} %broadcast_multiply_fusion.4) | copy-start | bytes 1540
  230.8 82.6 %copy-start.33 = (bf16[1,128,1,192]{1,3,2,0:T(8,128)(2,1)}, bf16[1,128,1,192]{1,3,2,0:T(8,128)(2,1)S(1)}, u32[]{:S(2)}) copy-start(bf16[1,128,1,192]{1,3,2,0:T(8,128)(2,1)S(1)} %slice.249) | copy-start | bytes 147460
  233.2 78.2 %copy-start.20 = (f32[1,128,768]{2,1,0:T(8,128)S(1)}, f32[1,128,768]{2,1,0:T(8,128)}, u32[]{:S(2)}) copy-start(f32[1,128,768]{2,1,0:T(8,128)} %param.37) | copy-start | bytes 1179652
  233.2 73.9 %all-reduce.18.cloned.1.call-start = ((), (), s32[]{:S(2)}) async-start(), calls=%async_computation.5 | async-start | bytes 393216 | tf_op jit(solution)/shard_map/psum | solution.py:56
  272.5 84.6 %copy-start.85 = (f32[128]{0:T(128)S(1)}, f32[128]{0:T(128)}, u32[]{:S(2)}) copy-start(f32[128]{0:T(128)} %copy-done.84) | copy-start | bytes 1540
  275.0 79.6 %all-reduce.20.cloned.1.call-start = ((), (), s32[]{:S(2)}) async-start(), calls=%async_computation.6 | async-start | bytes 393216 | tf_op jit(solution)/shard_map/psum | solution.py:56
  322.4 77.1 %copy-start.92 = (f32[128]{0:T(128)S(1)}, f32[128]{0:T(128)}, u32[]{:S(2)}) copy-start(f32[128]{0:T(128)} %copy-done.91) | copy-start | bytes 1540
  322.4 74.6 %all-reduce.22.cloned.1.call-start = ((), (), s32[]{:S(2)}) async-start(), calls=%async_computation.7 | async-start | bytes 393216 | tf_op jit(solution)/shard_map/psum | solution.py:56
  364.9 134.9 %all-reduce.24.cloned.1.call-start = ((), (), s32[]{:S(2)}) async-start(), calls=%async_computation.10 | async-start | bytes 786432 | tf_op jit(solution)/shard_map/psum | solution.py:52
  431.0 157.4 %all-gather.2.cloned.1.call-start = ((), (), s32[]{:S(2)}) async-start(), calls=%async_computation.8 | async-start | bytes 2949120 | tf_op jit(solution)/shard_map/all_gather | solution.py:163
  431.8 218.7 %reduce-scatter.4.cloned.1.call-start = ((), (), s32[]{:S(2)}) async-start(), calls=%async_computation.9 | async-start | bytes 7962624
  493.6 77.9 %all-to-all-start = ((bf16[1,6312,2,192]{3,2,0,1:T(2,128)(2,1)}), bf16[1,6312,2,192]{3,2,0,1:T(2,128)(2,1)}, u32[]{:S(2)}, u32[]{:S(2)}) async-start(bf16[1,6312,2,192]{3,2,0,1:T(2,128)(2,1)} %copy.59), calls=%async_computation | async-start | bytes 12926976 | tf_op jit(solution)/shard_map/all_to_all | solution.py:293
  (106 other events, 1496.2 us)
Sparse Core Ops, SparseCore 0:
  157.0 33.7 all-reduce.11
  196.8 32.0 all-reduce.13
  233.3 32.0 all-reduce.15
  275.1 31.9 all-reduce.17
  322.5 32.0 all-reduce.19
  365.0 31.9 all-reduce.21
  431.1 32.9 all-reduce.23
  465.6 24.0 all-gather.1
  493.4 129.8 reduce-scatter.3
